TPU v7x, 32 devices: a whole 2x2x4 slice. The times are simulated.
32 devices in a mesh: gx: 8 (over y, x, core), gy: 4 (over z).
Axes of the slice: x: 2, y: 2, z: 4, core: 2. Of those that a mesh axis runs over, the one named last changes fastest.
Arguments:
- layer_early: bfloat16 [1024, 8192], P(None, ('gx', 'gy')), may hold values from -48 to 48
- layer_late: bfloat16 [1024, 8192], P(('gx', 'gy')), may hold values from -48 to 48
Outputs:
- similarity: float32 [], replicated
- token_share: float32 [1024], P(('gx', 'gy'))
- early_rows: bfloat16 [1024, 8192], P(('gx', 'gy'))
- late_rows: bfloat16 [1024, 8192], P(('gx', 'gy'))
All inputs are finite; a program needn't handle non-finite values.
Results may differ from a plain program's by a relative error of at most 0.0015.
Values may be sent and summed in bfloat16 or wider, within the bound.
A program may use at most 128 MiB of HBM per device.

v0:
```python
import jax
import jax.numpy as jnp
from jax import lax
from jax.sharding import PartitionSpec as P


def pair_terms(left_early, left_late, right_early, right_late):
    dims = (((1,), (1,)), ((), ()))
    block_early = lax.dot_general(left_early, right_early, dims, preferred_element_type=jnp.float32)
    block_late = lax.dot_general(left_late, right_late, dims, preferred_element_type=jnp.float32)
    return (
        jnp.sum(block_early * block_late, axis=1),
        jnp.sum(block_early * block_early),
        jnp.sum(block_late * block_late),
    )


def body(layer_early, layer_late):
    total_rows = layer_early.shape[0]
    early_values = layer_early.astype(jnp.float32)
    early_cols = (early_values - jnp.mean(early_values, axis=0)).astype(jnp.bfloat16)
    late_values = layer_late.astype(jnp.float32)
    column_sums = lax.psum(jnp.sum(late_values, axis=0), ("gx", "gy"))
    late_rows = (late_values - column_sums / total_rows).astype(jnp.bfloat16)
    early_rows = lax.all_to_all(early_cols, ("gx", "gy"), split_axis=0, concat_axis=1, tiled=True)
    block_early, block_late = (
        lax.all_gather(early_rows, "gy", axis=0, tiled=True),
        lax.all_gather(late_rows, "gy", axis=0, tiled=True),
    )
    row_part, early_part, late_part = pair_terms(
        block_early,
        block_late,
        lax.all_gather(early_rows, "gx", axis=0, tiled=True),
        lax.all_gather(late_rows, "gx", axis=0, tiled=True),
    )
    own_align = lax.psum_scatter(row_part, "gy", scatter_dimension=0, tiled=True)
    total_kl, total_kk, total_ll = lax.psum(
        (jnp.sum(row_part), early_part, late_part), ("gx", "gy")
    )
    scale_norm = jnp.sqrt(total_kk * total_ll)
    similarity = total_kl / scale_norm
    token_share = total_rows * own_align / scale_norm
    return (similarity, token_share, early_rows, late_rows)


def solution(mesh):
    in_specs = (P(None, ("gx", "gy")), P(("gx", "gy"), None))
    out_specs = (P(), P(("gx", "gy")), P(("gx", "gy"), None), P(("gx", "gy"), None))
    return jax.shard_map(body, mesh=mesh, in_specs=in_specs, out_specs=out_specs, check_vma=False)
```

profile of v0, /device:TPU:0, one launch (start us, length us, event | category | flops | bytes accessed | tf_op | source)
XLA Modules:
  0.0 298.2 jit_solution(8457581897998979989)
XLA Ops:
  7.2 0.0 all-gather.9.cloned.1.call-start
  7.2 1.2 convert_reduce_fusion
  8.4 42.1 %psum.28 = f32[8192]{0:T(1024)S(1)} all-reduce(f32[8192]{0:T(1024)S(1)} %convert_reduce_fusion), channel_id=1, replica_groups=mesh['gx'=8,'gy'=4] {'gx','gy'}, use_global_device_ids=true, to_apply=%region_2.0 | all-reduce | flops 8192 | bytes 65536 | tf_op jit(solution)/shard_map/psum | solution.py:23
  50.6 1.9 fusion.1
  52.5 0.0 all-gather.11.cloned.1.call-start
  52.5 0.7 all-gather.11.cloned.1.call-update
  53.3 0.0 all-gather.5.cloned.1.call-start
  53.3 1.2 convert_reduce_fusion.1
  54.5 1.1 fusion
  55.6 28.2 %all_to_all.19 = bf16[32,32,256]{2,1,0:T(8,128)(2,1)S(1)} all-to-all(bf16[32,32,256]{2,1,0:T(8,128)(2,1)S(1)} %bitcast.12), channel_id=1, replica_groups=mesh['gx'=8,'gy'=4] {'gx','gy'}, dimensions={0} | all-to-all | bytes 1048576 | tf_op jit(solution)/shard_map/all_to_all | solution.py:25
  83.9 0.8 copy.8
  84.7 0.0 all-gather.5.cloned.1.call-update
  84.7 0.0 all-gather.7.cloned.1.call-start
  84.8 0.5 all-gather.7.cloned.1.call-update
  85.3 0.6 dynamic-slice
  86.6 22.4 %all-gather.9.cloned.1.call-done = bf16[128,8192]{1,0:T(8,128)(2,1)} async-done(((bf16[32,8192]{1,0:T(8,128)(2,1)}), bf16[128,8192]{1,0:T(8,128)(2,1)}) %all-gather.9.cloned.1.call-update) | async-done | bytes 2097168 | tf_op jit(solution)/shard_map/all_gather | solution.py:28
  109.0 38.1 %all-gather.11.cloned.1.call-done = bf16[256,8192]{1,0:T(8,128)(2,1)} async-done(((bf16[32,8192]{1,0:T(8,128)(2,1)}), bf16[256,8192]{1,0:T(8,128)(2,1)}) %all-gather.11.cloned.1.call-update) | async-done | bytes 4194320 | tf_op jit(solution)/shard_map/all_gather | solution.py:34
  147.1 4.4 %fusion.3 = f32[128,256]{1,0:T(8,128)S(1)} fusion(bf16[128,8192]{1,0:T(8,128)(2,1)} %all-gather.9.cloned.1.call-done, bf16[256,8192]{1,0:T(8,128)(2,1)} %all-gather.11.cloned.1.call-done), kind=kOutput, calls=%fused_computation.14 | convolution fusion | flops 536870912 | bytes 6422528 | tf_op jit(solution)/shard_map/dot_general | solution.py:10
  151.5 43.5 %all-gather.5.cloned.1.call-done = bf16[128,8192]{1,0:T(8,128)(2,1)} async-done(((bf16[32,8192]{1,0:T(8,128)(2,1)}), bf16[128,8192]{1,0:T(8,128)(2,1)}) %all-gather.5.cloned.1.call-update) | async-done | bytes 2097168 | tf_op jit(solution)/shard_map/all_gather | solution.py:27
  195.0 37.7 %all-gather.7.cloned.1.call-done = bf16[256,8192]{1,0:T(8,128)(2,1)} async-done(((bf16[32,8192]{1,0:T(8,128)(2,1)}), bf16[256,8192]{1,0:T(8,128)(2,1)}) %all-gather.7.cloned.1.call-update) | async-done | bytes 4194320 | tf_op jit(solution)/shard_map/all_gather | solution.py:33
  232.7 5.0 %multiply_reduce_fusion.2 = (f32[128]{0:T(128)S(1)}, f32[]{:T(128)}, f32[]{:T(128)}, f32[]{:T(128)}) fusion(f32[128,256]{1,0:T(8,128)S(1)} %fusion.3, bf16[128,8192]{1,0:T(8,128)(2,1)} %all-gather.5.cloned.1.call-done, bf16[256,8192]{1,0:T(8,128)(2,1)} %all-gather.7.cloned.1.call-done), kind=kOutput, calls=%fused_computation.8 | convolution fusion | flops 537100160 | bytes 6423052 | tf_op jit(solution)/shard_map/dot_general | solution.py:9
  237.7 39.6 %all-reduce.1 = (f32[]{:T(128)}, f32[]{:T(128)}, f32[]{:T(128)}) all-reduce(f32[]{:T(128)} %get-tuple-element.5, f32[]{:T(128)} %get-tuple-element.7, f32[]{:T(128)} %get-tuple-element.6), channel_id=1, replica_groups=mesh['gx'=8,'gy'=4] {'gx','gy'}, use_global_device_ids=true, to_apply=%region_4.0 | all-reduce | flops 3 | bytes 24 | tf_op jit(solution)/shard_map/psum | solution.py:37
  278.7 10.6 %all-reduce = f32[128]{0:T(128)S(1)} all-reduce(f32[128]{0:T(128)S(1)} %get-tuple-element.4), channel_id=2, replica_groups=mesh['gx'=8,'gy'=4] {'gy'}, use_global_device_ids=true, to_apply=%region_10.0.clone | all-reduce | flops 128 | bytes 1024
  290.0 0.6 fusion.2
  (5 shorter events, 0.0 us)
Async XLA Ops:
  7.2 78.2 %copy-start = (u32[32]{0:T(128)S(1)}, u32[32]{0:T(128)}, u32[]{:S(2)}) copy-start(u32[32]{0:T(128)} %constant.11) | copy-start | bytes 388
  7.2 101.8 %all-gather.9.cloned.1.call-start = ((), (), s32[]{:S(2)}) async-start(), calls=%async_computation.3 | async-start | bytes 2621440 | tf_op jit(solution)/shard_map/all_gather | solution.py:28
  52.5 94.6 %all-gather.11.cloned.1.call-start = ((), (), s32[]{:S(2)}) async-start(), calls=%async_computation.4 | async-start | bytes 4718592 | tf_op jit(solution)/shard_map/all_gather | solution.py:34
  53.3 141.7 %all-gather.5.cloned.1.call-start = ((), (), s32[]{:S(2)}) async-start(), calls=%async_computation.1 | async-start | bytes 2621440 | tf_op jit(solution)/shard_map/all_gather | solution.py:27
  84.7 147.9 %all-gather.7.cloned.1.call-start = ((), (), s32[]{:S(2)}) async-start(), calls=%async_computation.2 | async-start | bytes 4718592 | tf_op jit(solution)/shard_map/all_gather | solution.py:33
Sparse Core Ops, SparseCore 0:
  52.6 56.3 all-gather.8
  111.5 35.5 all-gather.10
  149.3 45.6 all-gather.4
  197.3 35.3 all-gather.6
where the time goes:
time: 299 us; the launch traced here: 298 us
  waiting for transfers between devices  143 us (48%)
  blocking collectives  121 us (40%)
  between operations  17.6 us (6%)
  matrix products  9.4 us (3%)
  other arithmetic  6.03 us (2%)
    all_gather x1, waiting for transfers between devices, body(): lax.all_gather(early_rows, 'gy', axis=0, tiled=True)  43.5 us
    psum x1, blocking collectives, body(): column_sums = lax.psum(jnp.sum(late_values, axis=0), ('gx', 'gy'))  42.1 us
    psum x1, blocking collectives, body(): lax.psum((jnp.sum(row_part), early_part, late_part), ('gx', 'gy'))  39.6 us
    all_gather x1, waiting for transfers between devices, body(): lax.all_gather(late_rows, 'gx', axis=0, tiled=True)  38.1 us
    all_gather x1, waiting for transfers between devices, body(): lax.all_gather(early_rows, 'gx', axis=0, tiled=True)  37.7 us
    all_to_all x1, blocking collectives, body(): lax.all_to_all(early_cols, ('gx', 'gy'), split_axis=0, concat_axis=1, til...  28.2 us
    all_gather x1, waiting for transfers between devices, body(): lax.all_gather(late_rows, 'gy', axis=0, tiled=True)  22.4 us
    unnamed x1, blocking collectives  10.6 us
  transfers between devices with their start and end apart: 4, of which 4 were waited for; matrix products, arithmetic and copies ran while one was open for 3% of the time, Pallas kernels for 0%

commit v1 on v0

--- a/solution.py
+++ b/solution.py
@@ -2,6 +2,12 @@
 import jax.numpy as jnp
 from jax import lax
 from jax.sharding import PartitionSpec as P
+
+
+def add_all(x, mesh_axis):
+    parts = lax.all_gather(x, mesh_axis, axis=0, tiled=False)
+    result = parts.sum(axis=0)
+    return result
 
 
 def pair_terms(left_early, left_late, right_early, right_late):
@@ -20,7 +26,7 @@
     early_values = layer_early.astype(jnp.float32)
     early_cols = (early_values - jnp.mean(early_values, axis=0)).astype(jnp.bfloat16)
     late_values = layer_late.astype(jnp.float32)
-    column_sums = lax.psum(jnp.sum(late_values, axis=0), ("gx", "gy"))
+    column_sums = add_all(jnp.sum(late_values, axis=0), ("gx", "gy"))
     late_rows = (late_values - column_sums / total_rows).astype(jnp.bfloat16)
     early_rows = lax.all_to_all(early_cols, ("gx", "gy"), split_axis=0, concat_axis=1, tiled=True)
     block_early, block_late = (

time: 299 us -> 314 us (1.050)
  waiting for transfers between devices: 143 us -> 204 us
  blocking collectives: 121 us -> 75 us
    all_gather x0 -> x1, waiting for transfers between devices: none -> 59 us  [add_all(): parts = lax.all_gather(x, mesh_axis, axis=0, tiled=False)]
    psum x1 -> x0, blocking collectives: 42.1 us -> none  [body(): column_sums = lax.psum(jnp.sum(late_values, axis=0), ('gx', 'gy'))]
    all_to_all x1, blocking collectives: 28.2 us -> 24.8 us  [body(): lax.all_to_all(early_cols, ('gx', 'gy'), split_axis=0, concat_axis=1, til...]
  transfers between devices with their start and end apart: 4 -> 5, of which waited for: 4 -> 5; matrix products, arithmetic and copies ran while one was open for 3% -> 2% of each run, Pallas kernels for 0% -> 0%
where the time goes in v1:
time: 314 us; the launch traced here: 313 us
  waiting for transfers between devices  204 us (65%)
  blocking collectives  75 us (24%)
  between operations  17.7 us (6%)
  matrix products  9.4 us (3%)
  other arithmetic  3.69 us (1%)
    all_gather x1, waiting for transfers between devices, add_all(): parts = lax.all_gather(x, mesh_axis, axis=0, tiled=False)  59 us
    all_gather x1, waiting for transfers between devices, body(): lax.all_gather(early_rows, 'gy', axis=0, tiled=True)  43.3 us
    psum x1, blocking collectives, body(): lax.psum((jnp.sum(row_part), early_part, late_part), ('gx', 'gy'))  39.6 us
    all_gather x1, waiting for transfers between devices, body(): lax.all_gather(late_rows, 'gx', axis=0, tiled=True)  38.1 us
    all_gather x1, waiting for transfers between devices, body(): lax.all_gather(early_rows, 'gx', axis=0, tiled=True)  37.7 us
    all_gather x1, waiting for transfers between devices, body(): lax.all_gather(late_rows, 'gy', axis=0, tiled=True)  25.1 us
    all_to_all x1, blocking collectives, body(): lax.all_to_all(early_cols, ('gx', 'gy'), split_axis=0, concat_axis=1, til...  24.8 us
    unnamed x1, blocking collectives  10.6 us
  transfers between devices with their start and end apart: 5, of which 5 were waited for; matrix products, arithmetic and copies ran while one was open for 2% of the time, Pallas kernels for 0%

profile of v1, /device:TPU:0, one launch (start us, length us, event | category | flops | bytes accessed | tf_op | source)
XLA Modules:
  0.0 313.2 jit_solution(8967454609239562166)
XLA Ops:
  7.2 1.9 convert_reduce_fusion
  9.1 0.0 all-gather.11.cloned.1.call-start
  9.2 59.0 %all-gather.15.cloned.1.call-done = f32[262144]{0:T(1024)} async-done(((f32[8192]{0:T(1024)}), f32[262144]{0:T(1024)}) %all-gather.15.cloned.1.call-update) | async-done | bytes 1048592 | tf_op jit(solution)/shard_map/all_gather | solution.py:8
  68.1 1.4 reshape.17
  69.5 0.1 reduce_sum.65
  69.7 0.9 fusion.1
  70.6 0.0 all-gather.13.cloned.1.call-start
  70.6 0.7 all-gather.13.cloned.1.call-update
  71.4 0.2 convert_reduce_fusion.1
  71.5 0.1 fusion
  71.7 24.8 %all_to_all.19 = bf16[32,32,256]{2,1,0:T(8,128)(2,1)S(1)} all-to-all(bf16[32,32,256]{2,1,0:T(8,128)(2,1)S(1)} %bitcast.12), channel_id=1, replica_groups=mesh['gx'=8,'gy'=4] {'gx','gy'}, dimensions={0} | all-to-all | bytes 1048576 | tf_op jit(solution)/shard_map/all_to_all | solution.py:31
  96.5 0.8 copy.9
  97.3 0.0 all-gather.9.cloned.1.call-start
  97.4 0.5 all-gather.9.cloned.1.call-update
  97.9 0.6 dynamic-slice
  99.1 25.1 %all-gather.11.cloned.1.call-done = bf16[128,8192]{1,0:T(8,128)(2,1)} async-done(((bf16[32,8192]{1,0:T(8,128)(2,1)}), bf16[128,8192]{1,0:T(8,128)(2,1)}) %all-gather.11.cloned.1.call-update) | async-done | bytes 2097168 | tf_op jit(solution)/shard_map/all_gather | solution.py:34
  124.2 38.1 %all-gather.13.cloned.1.call-done = bf16[256,8192]{1,0:T(8,128)(2,1)} async-done(((bf16[32,8192]{1,0:T(8,128)(2,1)}), bf16[256,8192]{1,0:T(8,128)(2,1)}) %all-gather.13.cloned.1.call-update) | async-done | bytes 4194320 | tf_op jit(solution)/shard_map/all_gather | solution.py:40
  162.3 4.4 %fusion.3 = f32[128,256]{1,0:T(8,128)S(1)} fusion(bf16[128,8192]{1,0:T(8,128)(2,1)} %all-gather.11.cloned.1.call-done, bf16[256,8192]{1,0:T(8,128)(2,1)} %all-gather.13.cloned.1.call-done), kind=kOutput, calls=%fused_computation.14 | convolution fusion | flops 536870912 | bytes 6422528 | tf_op jit(solution)/shard_map/dot_general | solution.py:16
  166.7 43.3 %all-gather.7.cloned.1.call-done = bf16[128,8192]{1,0:T(8,128)(2,1)} async-done(((bf16[32,8192]{1,0:T(8,128)(2,1)}), bf16[128,8192]{1,0:T(8,128)(2,1)}) %all-gather.7.cloned.1.call-update) | async-done | bytes 2097168 | tf_op jit(solution)/shard_map/all_gather | solution.py:33
  210.0 37.7 %all-gather.9.cloned.1.call-done = bf16[256,8192]{1,0:T(8,128)(2,1)} async-done(((bf16[32,8192]{1,0:T(8,128)(2,1)}), bf16[256,8192]{1,0:T(8,128)(2,1)}) %all-gather.9.cloned.1.call-update) | async-done | bytes 4194320 | tf_op jit(solution)/shard_map/all_gather | solution.py:39
  247.7 5.0 %multiply_reduce_fusion.2 = (f32[128]{0:T(128)S(1)}, f32[]{:T(128)}, f32[]{:T(128)}, f32[]{:T(128)}) fusion(f32[128,256]{1,0:T(8,128)S(1)} %fusion.3, bf16[128,8192]{1,0:T(8,128)(2,1)} %all-gather.7.cloned.1.call-done, bf16[256,8192]{1,0:T(8,128)(2,1)} %all-gather.9.cloned.1.call-done), kind=kOutput, calls=%fused_computation.8 | convolution fusion | flops 537100160 | bytes 6423052 | tf_op jit(solution)/shard_map/dot_general | solution.py:15
  252.8 39.6 %all-reduce.1 = (f32[]{:T(128)}, f32[]{:T(128)}, f32[]{:T(128)}) all-reduce(f32[]{:T(128)} %get-tuple-element.5, f32[]{:T(128)} %get-tuple-element.7, f32[]{:T(128)} %get-tuple-element.6), channel_id=1, replica_groups=mesh['gx'=8,'gy'=4] {'gx','gy'}, use_global_device_ids=true, to_apply=%region_4.0 | all-reduce | flops 3 | bytes 24 | tf_op jit(solution)/shard_map/psum | solution.py:43
  293.7 10.6 %all-reduce = f32[128]{0:T(128)S(1)} all-reduce(f32[128]{0:T(128)S(1)} %get-tuple-element.4), channel_id=3, replica_groups=mesh['gx'=8,'gy'=4] {'gy'}, use_global_device_ids=true, to_apply=%region_10.0.clone | all-reduce | flops 128 | bytes 1024
  305.0 0.6 fusion.2
  (13 shorter events, 0.2 us)
Async XLA Ops:
  7.2 62.5 %copy-start.1 = (bf16[32,8192]{1,0:T(8,128)(2,1)S(1)}, bf16[32,8192]{1,0:T(8,128)(2,1)}, u32[]{:S(2)}) copy-start(bf16[32,8192]{1,0:T(8,128)(2,1)} %param.3) | copy-start | bytes 1572868
  7.2 64.2 %copy-start = (bf16[1024,256]{1,0:T(8,128)(2,1)S(1)}, bf16[1024,256]{1,0:T(8,128)(2,1)}, u32[]{:S(2)}) copy-start(bf16[1024,256]{1,0:T(8,128)(2,1)} %param.2) | copy-start | bytes 1572868
  7.2 60.9 %all-gather.15.cloned.1.call-start = ((), (), s32[]{:S(2)}) async-start(), calls=%async_computation.5 | async-start | bytes 1081344 | tf_op jit(solution)/shard_map/all_gather | solution.py:8
  9.1 115.1 %all-gather.11.cloned.1.call-start = ((), (), s32[]{:S(2)}) async-start(), calls=%async_computation.3 | async-start | bytes 2621440 | tf_op jit(solution)/shard_map/all_gather | solution.py:34
  69.5 28.4 %copy-start.2 = (u32[32]{0:T(128)S(1)}, u32[32]{0:T(128)}, u32[]{:S(2)}) copy-start(u32[32]{0:T(128)} %constant.11) | copy-start | bytes 388
  70.6 91.7 %all-gather.13.cloned.1.call-start = ((), (), s32[]{:S(2)}) async-start(), calls=%async_computation.4 | async-start | bytes 4718592 | tf_op jit(solution)/shard_map/all_gather | solution.py:40
  71.3 138.7 %all-gather.7.cloned.1.call-start = ((), (), s32[]{:S(2)}) async-start(), calls=%async_computation.1 | async-start | bytes 2621440 | tf_op jit(solution)/shard_map/all_gather | solution.py:33
  97.3 150.4 %all-gather.9.cloned.1.call-start = ((), (), s32[]{:S(2)}) async-start(), calls=%async_computation.2 | async-start | bytes 4718592 | tf_op jit(solution)/shard_map/all_gather | solution.py:39
Sparse Core Ops, SparseCore 0:
  11.6 56.5 all-gather.14
  70.7 53.4 all-gather.10
  126.7 35.5 all-gather.12
  164.3 45.6 all-gather.6
  212.3 35.3 all-gather.8
